TPU v7x, 32 devices: a whole 2x2x4 slice. The times are simulated.
32 devices in a mesh: blk: 8 (over y, x, core), grp: 4 (over z).
Axes of the slice: x: 2, y: 2, z: 4, core: 2. Of those that a mesh axis runs over, the one named last changes fastest.
Arguments:
- amplitudes: bfloat16 [896, 4, 896], P('blk', None, 'grp'), may hold values from -6 to 6
- grid_factor: bfloat16 [1024, 896], P(('blk', 'grp')), may hold values from -0.1875 to 0.1875
- metric: float32 [1024, 4, 256], P('blk', 'grp'), may hold values from -6 to 6
- virt_energy: float32 [896], replicated, may hold values from 0.2 to 4
- pair_energy: float32 [4], replicated, may hold values from -2 to -0.5
Outputs:
- residual: float32 [896, 4, 896], P('blk', None, 'grp')
All inputs are finite; a program needn't handle non-finite values.
Results may differ from a plain program's by a relative error of at most 0.005.
Values may be sent and summed in bfloat16 or wider, within the bound.
A program may use at most 64 MiB of HBM per device.

v0:
```python
import jax
import jax.numpy as jnp
from jax import lax
from jax.sharding import PartitionSpec as P


def local(amplitudes, grid_factor, metric, virt_energy, pair_energy):
    row_factor = lax.all_gather(grid_factor, "grp", axis=0, tiled=True)
    column_factor = lax.all_gather(grid_factor, "blk", axis=0, tiled=True)
    amplitude_rows = lax.all_gather(amplitudes, "blk", axis=0, tiled=True)
    row_count = row_factor.shape[0]
    left_part = jnp.einsum(
        "pc,ckd->kpd", row_factor, amplitude_rows, preferred_element_type=jnp.float32
    ).astype(jnp.bfloat16)
    columns = column_factor
    products = jnp.einsum(
        "kpd,qd->kpq",
        lax.all_gather(left_part, "grp", axis=2, tiled=True),
        columns,
        preferred_element_type=jnp.float32,
    )
    weighted = (metric.reshape(row_count, -1)[None] * products).astype(jnp.bfloat16)
    columns = column_factor
    mixed = lax.psum_scatter(
        jnp.einsum("kpq,qb->bkp", weighted, columns, preferred_element_type=jnp.float32).astype(
            jnp.bfloat16
        ),
        "grp",
        scatter_dimension=0,
        tiled=True,
    )
    columns = row_factor
    ladder = lax.psum_scatter(
        jnp.einsum("pa,bkp->akb", columns, mixed, preferred_element_type=jnp.float32).astype(
            jnp.bfloat16
        ),
        "blk",
        scatter_dimension=0,
        tiled=True,
    ).astype(jnp.float32)
    first_energy = lax.dynamic_slice_in_dim(
        virt_energy, lax.axis_index("blk") * amplitudes.shape[0], amplitudes.shape[0]
    )
    second_energy = lax.dynamic_slice_in_dim(
        virt_energy, lax.axis_index("grp") * amplitudes.shape[2], amplitudes.shape[2]
    )
    denominator = (
        first_energy[:, None, None] + second_energy[None, None, :] - pair_energy[None, :, None]
    )
    return denominator * amplitudes.astype(jnp.float32) + ladder


def solution(mesh):
    in_specs = (P("blk", None, "grp"), P(("blk", "grp"), None), P("blk", "grp", None), P(), P())
    out_specs = P("blk", None, "grp")
    return jax.shard_map(local, mesh=mesh, in_specs=in_specs, out_specs=out_specs, check_vma=False)
```

profile of v0, /device:TPU:0, one launch (start us, length us, event | category | flops | bytes accessed | tf_op | source)
XLA Modules:
  0.0 138.9 jit_solution(9741608353748779387)
XLA Ops:
  6.5 0.7 all-gather.2.cloned.1.call-update
  7.3 0.0 reduce-scatter.5.cloned.1.call-start
  7.3 0.9 copy.23
  8.2 15.7 %all_gather.13 = bf16[128,896]{1,0:T(8,128)(2,1)S(1)} all-gather(bf16[32,896]{1,0:T(8,128)(2,1)} %param.6), channel_id=1, replica_groups=mesh['blk'=8,'grp'=4] {'grp'}, dimensions={0}, use_global_device_ids=true | all-gather | bytes 286720 | tf_op jit(solution)/shard_map/all_gather | solution.py:8
  24.0 11.1 %all_gather.15 = bf16[256,896]{1,0:T(8,128)(2,1)S(1)} all-gather(bf16[32,896]{1,0:T(8,128)(2,1)} %param.6), channel_id=1, replica_groups=mesh['blk'=8,'grp'=4] {'blk'}, dimensions={0}, use_global_device_ids=true | all-gather | bytes 516096 | tf_op jit(solution)/shard_map/all_gather | solution.py:9
  35.0 4.2 %all-gather.2.cloned.1.call-done = bf16[896,4,224]{2,1,0:T(4,128)(2,1)} async-done(((bf16[112,4,224]{2,1,0:T(4,128)(2,1)}), bf16[896,4,224]{2,1,0:T(4,128)(2,1)}) %all-gather.2.cloned.1.call-update) | async-done | bytes 1605648 | tf_op jit(solution)/shard_map/all_gather | solution.py:10
  39.3 2.2 %fusion.7 = bf16[4,128,224]{1,2,0:T(8,128)(2,1)S(1)} fusion(bf16[896,4,224]{2,1,0:T(4,128)(2,1)} %all-gather.2.cloned.1.call-done, bf16[128,896]{1,0:T(8,128)(2,1)S(1)} %all_gather.13), kind=kOutput, calls=%fused_computation.8 | convolution fusion | flops 205635584 | bytes 2064384 | tf_op jit(solution)/shard_map/pc,ckd->kpd/dot_general | solution.py:12
  41.5 21.0 %all_gather.14 = bf16[4,128,896]{1,2,0:T(8,128)(2,1)S(1)} all-gather(bf16[4,128,224]{1,2,0:T(8,128)(2,1)S(1)} %fusion.7), channel_id=1, replica_groups=mesh['blk'=8,'grp'=4] {'grp'}, dimensions={2}, use_global_device_ids=true | all-gather | bytes 1146880 | tf_op jit(solution)/shard_map/all_gather | solution.py:18
  62.5 2.2 %fusion.2 = bf16[896,4,128]{2,0,1:T(8,128)(2,1)} fusion(bf16[4,128,896]{1,2,0:T(8,128)(2,1)S(1)} %all_gather.14, bf16[256,896]{1,0:T(8,128)(2,1)S(1)} %all_gather.15, f32[128,256]{1,0:T(8,128)S(1)} %bitcast.25), kind=kOutput, calls=%fused_computation.4 | convolution fusion | flops 470482944 | bytes 2424832 | tf_op jit(solution)/shard_map/kpq,qb->bkp/dot_general | solution.py:25
  64.7 0.0 reduce-scatter.5.cloned.1.call-update
  64.7 0.0 reduce-scatter.7.cloned.1.call-start
  64.8 24.3 %reduce-scatter.5.cloned.1.call-done = bf16[224,4,128]{2,0,1:T(8,128)(2,1)} async-done(((bf16[896,4,128]{2,0,1:T(8,128)(2,1)}), bf16[224,4,128]{2,0,1:T(8,128)(2,1)}) %reduce-scatter.5.cloned.1.call-update) | async-done | bytes 229392 | tf_op jit(solution)/shard_map/reduce_scatter | solution.py:24
  89.1 1.5 %convolution_convert_fusion = bf16[224,4,896]{2,0,1:T(8,128)(2,1)S(1)} fusion(bf16[224,4,128]{2,0,1:T(8,128)(2,1)} %reduce-scatter.5.cloned.1.call-done, bf16[128,896]{1,0:T(8,128)(2,1)S(1)} %all_gather.13), kind=kOutput, calls=%fused_computation.2 | convolution fusion | flops 206323712 | bytes 2064384 | tf_op jit(solution)/shard_map/pa,bkp->akb/dot_general | solution.py:34
  90.6 0.0 copy-start
  90.6 2.3 %copy.13 = bf16[896,896]{1,0:T(8,128)(2,1)} copy(bf16[896,896]{0,1:T(8,128)(2,1)S(1)} %bitcast.23) | data formatting | bytes 3211264
  92.9 0.0 reduce-scatter.7.cloned.1.call-update
  93.0 0.2 copy.8
  93.2 0.8 dynamic_slice.7
  93.9 0.8 dynamic_slice.6
  94.7 0.1 broadcast_add_fusion
  94.8 35.4 %reduce-scatter.7.cloned.1.call-done = bf16[112,896]{1,0:T(8,128)(2,1)} async-done(((bf16[896,896]{1,0:T(8,128)(2,1)}), bf16[112,896]{1,0:T(8,128)(2,1)}) %reduce-scatter.7.cloned.1.call-update) | async-done | bytes 200720
  130.2 1.1 copy.14
  131.3 0.2 convert_add_fusion
  131.4 1.0 copy.9
  (4 shorter events, 0.0 us)
Async XLA Ops:
  6.5 32.7 %all-gather.2.cloned.1.call-start = ((), (), s32[]{:S(2)}) async-start(), calls=%async_computation.2 | async-start | bytes 2064384 | tf_op jit(solution)/shard_map/all_gather | solution.py:10
  7.3 81.8 %reduce-scatter.5.cloned.1.call-start = ((), (), s32[]{:S(2)}) async-start(), calls=%async_computation.3 | async-start | bytes 1146880 | tf_op jit(solution)/shard_map/reduce_scatter | solution.py:24
  64.7 65.4 %reduce-scatter.7.cloned.1.call-start = ((), (), s32[]{:S(2)}) async-start(), calls=%async_computation.4 | async-start | bytes 1806336
  90.6 2.4 %copy-start = (bf16[112,4,224]{2,1,0:T(4,128)(2,1)S(1)}, bf16[112,4,224]{2,1,0:T(4,128)(2,1)}, u32[]{:S(2)}) copy-start(bf16[112,4,224]{2,1,0:T(4,128)(2,1)} %param.5) | copy-start | bytes 602116
  92.9 38.3 %copy-start.1 = (f32[4]{0:T(128)S(1)}, f32[4]{0:T(128)}, u32[]{:S(2)}) copy-start(f32[4]{0:T(128)} %param.9) | copy-start | bytes 52
Sparse Core Ops, SparseCore 0:
  9.2 30.0 all-gather.1
  64.8 24.2 reduce-scatter.4
  93.1 37.0 reduce-scatter.6
where the time goes:
time: 139 us
  waiting for transfers between devices  64.7 us (47%)
  blocking collectives  47.8 us (34%)
  between operations  13.2 us (9%)
  local copies, waits for them, and re-layouts  7.03 us (5%)
  matrix products  5.9 us (4%)
    unnamed x4, waiting for transfers between devices  36.1 us
    reduce_scatter x1, waiting for transfers between devices, local(): lax.psum_scatter(jnp.einsum('kpq,qb->bkp', weighted, columns, preferred_e...  24.3 us
    all_gather x1, blocking collectives, local(): lax.all_gather(left_part, 'grp', axis=2, tiled=True)  21 us
    all_gather x1, blocking collectives, local(): row_factor = lax.all_gather(grid_factor, 'grp', axis=0, tiled=True)  15.7 us
    all_gather x1, blocking collectives, local(): column_factor = lax.all_gather(grid_factor, 'blk', axis=0, tiled=True)  11.1 us
    unnamed x8, local copies, waits for them, and re-layouts  4.55 us
    all_gather x1, waiting for transfers between devices, local(): amplitude_rows = lax.all_gather(amplitudes, 'blk', axis=0, tiled=True)  4.22 us
  transfers between devices with their start and end apart: 3, of which 3 were waited for; matrix products, arithmetic and copies ran while one was open for 2% of the time, Pallas kernels for 0%

commit v1 on v0

--- a/solution.py
+++ b/solution.py
@@ -6,7 +6,12 @@
 
 def local(amplitudes, grid_factor, metric, virt_energy, pair_energy):
     row_factor = lax.all_gather(grid_factor, "grp", axis=0, tiled=True)
-    column_factor = lax.all_gather(grid_factor, "blk", axis=0, tiled=True)
+    ring = [grid_factor]
+    for hop in range(7):
+        ring.append(lax.ppermute(ring[-1], "blk", [(dev, (dev + 1) % 8) for dev in range(8)]))
+    column_factor = jnp.roll(
+        jnp.concatenate(ring[::-1], axis=0), (lax.axis_index("blk") + 1) * ring[0].shape[0], axis=0
+    )
     amplitude_rows = lax.all_gather(amplitudes, "blk", axis=0, tiled=True)
     row_count = row_factor.shape[0]
     left_part = jnp.einsum(

time: 139 us -> 152 us (1.094)
  waiting for transfers between devices: 64.7 us -> 89.9 us
  blocking collectives: 47.8 us -> 33.8 us
    ppermute x0 -> x7, waiting for transfers between devices: none -> 27.7 us  [local(): lax.ppermute(ring[-1], 'blk', [(dev, (dev + 1) % 8) for dev in range(8)])]
    all_gather x1 -> x0, blocking collectives: 11.1 us -> none  [local(): column_factor = lax.all_gather(grid_factor, 'blk', axis=0, tiled=True)]
    all_gather x1, waiting for transfers between devices: 4.22 us -> 0.02 us  [local(): amplitude_rows = lax.all_gather(amplitudes, 'blk', axis=0, tiled=True)]
    all_gather x1, blocking collectives: 21 us -> 18.3 us  [local(): lax.all_gather(left_part, 'grp', axis=2, tiled=True)]
    reduce_scatter x1, waiting for transfers between devices: 24.3 us -> 26.1 us  [local(): lax.psum_scatter(jnp.einsum('kpq,qb->bkp', weighted, columns, preferred_e...]
    unnamed x8 -> x25, local copies, waits for them, and re-layouts: 4.55 us -> 5.58 us
  transfers between devices with their start and end apart: 3 -> 10, of which waited for: 3 -> 8; matrix products, arithmetic and copies ran while one was open for 2% -> 2% of each run, Pallas kernels for 0% -> 0%
where the time goes in v1:
time: 152 us
  waiting for transfers between devices  89.9 us (59%)
  blocking collectives  33.8 us (22%)
  between operations  13.3 us (9%)
  local copies, waits for them, and re-layouts  8.08 us (5%)
  matrix products  5.93 us (4%)
    unnamed x4, waiting for transfers between devices  36.1 us
    ppermute x7, waiting for transfers between devices, local(): lax.ppermute(ring[-1], 'blk', [(dev, (dev + 1) % 8) for dev in range(8)])  27.7 us
    reduce_scatter x1, waiting for transfers between devices, local(): lax.psum_scatter(jnp.einsum('kpq,qb->bkp', weighted, columns, preferred_e...  26.1 us
    all_gather x1, blocking collectives, local(): lax.all_gather(left_part, 'grp', axis=2, tiled=True)  18.3 us
    all_gather x1, blocking collectives, local(): row_factor = lax.all_gather(grid_factor, 'grp', axis=0, tiled=True)  15.5 us
    unnamed x25, local copies, waits for them, and re-layouts  5.58 us
  transfers between devices with their start and end apart: 10, of which 8 were waited for; matrix products, arithmetic and copies ran while one was open for 2% of the time, Pallas kernels for 0%

profile of v1, /device:TPU:0, one launch (start us, length us, event | category | flops | bytes accessed | tf_op | source)
XLA Modules:
  0.0 151.8 jit_solution(14834468227192587217)
XLA Ops:
  6.5 0.7 all-gather.2.cloned.1.call-update
  7.3 0.5 collective-permute-start
  7.8 4.9 %collective-permute-done = bf16[32,896]{1,0:T(8,128)(2,1)S(1)} collective-permute-done((bf16[32,896]{1,0:T(8,128)(2,1)}, bf16[32,896]{1,0:T(8,128)(2,1)S(1)}, u32[]{:S(2)}, u32[]{:S(2)}) %collective-permute-start) | collective-permute-done | bytes 57376 | tf_op jit(solution)/shard_map/ppermute | solution.py:11
  12.8 4.5 %collective-permute-done.1 = bf16[32,896]{1,0:T(8,128)(2,1)S(1)} collective-permute-done((bf16[32,896]{1,0:T(8,128)(2,1)S(1)}, bf16[32,896]{1,0:T(8,128)(2,1)S(1)}, u32[]{:S(2)}, u32[]{:S(2)}) %collective-permute-start.1) | collective-permute-done | bytes 57376 | tf_op jit(solution)/shard_map/ppermute | solution.py:11
  17.3 4.5 %collective-permute-done.2 = bf16[32,896]{1,0:T(8,128)(2,1)S(1)} collective-permute-done((bf16[32,896]{1,0:T(8,128)(2,1)S(1)}, bf16[32,896]{1,0:T(8,128)(2,1)S(1)}, u32[]{:S(2)}, u32[]{:S(2)}) %collective-permute-start.2) | collective-permute-done | bytes 57376 | tf_op jit(solution)/shard_map/ppermute | solution.py:11
  21.8 4.5 %collective-permute-done.3 = bf16[32,896]{1,0:T(8,128)(2,1)S(1)} collective-permute-done((bf16[32,896]{1,0:T(8,128)(2,1)S(1)}, bf16[32,896]{1,0:T(8,128)(2,1)S(1)}, u32[]{:S(2)}, u32[]{:S(2)}) %collective-permute-start.3) | collective-permute-done | bytes 57376 | tf_op jit(solution)/shard_map/ppermute | solution.py:11
  26.3 4.5 %collective-permute-done.4 = bf16[32,896]{1,0:T(8,128)(2,1)S(1)} collective-permute-done((bf16[32,896]{1,0:T(8,128)(2,1)S(1)}, bf16[32,896]{1,0:T(8,128)(2,1)S(1)}, u32[]{:S(2)}, u32[]{:S(2)}) %collective-permute-start.4) | collective-permute-done | bytes 57376 | tf_op jit(solution)/shard_map/ppermute | solution.py:11
  30.8 0.9 copy.23
  31.7 4.8 %collective-permute-done.5 = bf16[32,896]{1,0:T(8,128)(2,1)S(1)} collective-permute-done((bf16[32,896]{1,0:T(8,128)(2,1)S(1)}, bf16[32,896]{1,0:T(8,128)(2,1)S(1)}, u32[]{:S(2)}, u32[]{:S(2)}) %collective-permute-start.5) | collective-permute-done | bytes 57376 | tf_op jit(solution)/shard_map/ppermute | solution.py:11
  36.5 15.5 %all_gather.10 = bf16[128,896]{1,0:T(8,128)(2,1)S(1)} all-gather(bf16[32,896]{1,0:T(8,128)(2,1)} %param.6), channel_id=1, replica_groups=mesh['blk'=8,'grp'=4] {'grp'}, dimensions={0}, use_global_device_ids=true | all-gather | bytes 286720 | tf_op jit(solution)/shard_map/all_gather | solution.py:8
  52.1 0.8 constant_dynamic-update-slice_fusion.8
  53.1 2.2 %fusion.6 = bf16[4,128,224]{1,2,0:T(8,128)(2,1)S(1)} fusion(bf16[896,4,224]{2,1,0:T(4,128)(2,1)} %all-gather.2.cloned.1.call-done, bf16[128,896]{1,0:T(8,128)(2,1)S(1)} %all_gather.10), kind=kOutput, calls=%fused_computation.7 | convolution fusion | flops 205635584 | bytes 2064384 | tf_op jit(solution)/shard_map/pc,ckd->kpd/dot_general | solution.py:17
  55.3 18.3 %all_gather.11 = bf16[4,128,896]{1,2,0:T(8,128)(2,1)S(1)} all-gather(bf16[4,128,224]{1,2,0:T(8,128)(2,1)S(1)} %fusion.6), channel_id=1, replica_groups=mesh['blk'=8,'grp'=4] {'grp'}, dimensions={2}, use_global_device_ids=true | all-gather | bytes 1146880 | tf_op jit(solution)/shard_map/all_gather | solution.py:23
  73.7 2.2 %convolution_convert_fusion.1 = bf16[896,4,128]{2,0,1:T(8,128)(2,1)} fusion(bf16[4,128,896]{1,2,0:T(8,128)(2,1)S(1)} %all_gather.11, bf16[512,896]{1,0:T(8,128)(2,1)S(1)} %constant_dynamic-update-slice_fusion, s32[]{:T(128)S(6)} %select_n.22, f32[128,256]{1,0:T(8,128)S(1)} %bitcast.23), kind=kOutput, calls=%fused_computation.3 | convolution fusion | flops 470482944 | bytes 2884608 | tf_op jit(solution)/shard_map/kpq,qb->bkp/dot_general | solution.py:30
  75.9 26.1 %reduce-scatter.5.cloned.1.call-done = bf16[224,4,128]{2,0,1:T(8,128)(2,1)} async-done(((bf16[896,4,128]{2,0,1:T(8,128)(2,1)}), bf16[224,4,128]{2,0,1:T(8,128)(2,1)}) %reduce-scatter.5.cloned.1.call-update) | async-done | bytes 229392 | tf_op jit(solution)/shard_map/reduce_scatter | solution.py:29
  102.0 1.5 convolution_convert_fusion
  103.5 2.3 %copy.13 = bf16[896,896]{1,0:T(8,128)(2,1)} copy(bf16[896,896]{0,1:T(8,128)(2,1)S(1)} %bitcast.21) | data formatting | bytes 3211264
  105.9 0.2 copy.8
  106.1 0.8 dynamic_slice.10
  106.9 0.8 dynamic_slice.11
  107.7 35.3 %reduce-scatter.7.cloned.1.call-done = bf16[112,896]{1,0:T(8,128)(2,1)} async-done(((bf16[896,896]{1,0:T(8,128)(2,1)}), bf16[112,896]{1,0:T(8,128)(2,1)}) %reduce-scatter.7.cloned.1.call-update) | async-done | bytes 200720
  143.1 1.1 copy.14
  144.2 0.2 convert_add_fusion
  144.3 1.0 copy.9
  (35 shorter events, 0.4 us)
Async XLA Ops:
  6.5 46.5 %copy-start.1 = (bf16[32,896]{1,0:T(8,128)(2,1)S(1)}, bf16[32,896]{1,0:T(8,128)(2,1)}, u32[]{:S(2)}) copy-start(bf16[32,896]{1,0:T(8,128)(2,1)} %param.6) | copy-start | bytes 172036
  6.5 46.5 %all-gather.2.cloned.1.call-start = ((), (), s32[]{:S(2)}) async-start(), calls=%async_computation.2 | async-start | bytes 2064384 | tf_op jit(solution)/shard_map/all_gather | solution.py:15
  7.3 94.7 %reduce-scatter.5.cloned.1.call-start = ((), (), s32[]{:S(2)}) async-start(), calls=%async_computation.3 | async-start | bytes 1146880 | tf_op jit(solution)/shard_map/reduce_scatter | solution.py:29
  7.3 5.5 %collective-permute-start = (bf16[32,896]{1,0:T(8,128)(2,1)}, bf16[32,896]{1,0:T(8,128)(2,1)S(1)}, u32[]{:S(2)}, u32[]{:S(2)}) collective-permute-start(bf16[32,896]{1,0:T(8,128)(2,1)} %param.6), channel_id=1, source_target_pairs={{0,4},{4,8},{8,12},{12,16},{16,20},{20,24},{24,28},{28,0},{1,5},{5... | collective-permute-start | bytes 172040 | tf_op jit(solution)/shard_map/ppermute | solution.py:11
  12.8 4.5 %collective-permute-start.1 = (bf16[32,896]{1,0:T(8,128)(2,1)S(1)}, bf16[32,896]{1,0:T(8,128)(2,1)S(1)}, u32[]{:S(2)}, u32[]{:S(2)}) collective-permute-start(bf16[32,896]{1,0:T(8,128)(2,1)S(1)} %collective-permute-done), channel_id=1, source_target_pairs={{0,4},{4,8},{8,12},{12,16},{16,20},{20,24},{24,28},{28,0},{1,5},{5... | collective-permute-start | bytes 172040 | tf_op jit(solution)/shard_map/ppermute | solution.py:11
  17.3 4.5 %collective-permute-start.2 = (bf16[32,896]{1,0:T(8,128)(2,1)S(1)}, bf16[32,896]{1,0:T(8,128)(2,1)S(1)}, u32[]{:S(2)}, u32[]{:S(2)}) collective-permute-start(bf16[32,896]{1,0:T(8,128)(2,1)S(1)} %collective-permute-done.1), channel_id=1, source_target_pairs={{0,4},{4,8},{8,12},{12,16},{16,20},{20,24},{24,28},{28,0},{1,5},{5... | collective-permute-start | bytes 172040 | tf_op jit(solution)/shard_map/ppermute | solution.py:11
  21.8 4.5 %collective-permute-start.3 = (bf16[32,896]{1,0:T(8,128)(2,1)S(1)}, bf16[32,896]{1,0:T(8,128)(2,1)S(1)}, u32[]{:S(2)}, u32[]{:S(2)}) collective-permute-start(bf16[32,896]{1,0:T(8,128)(2,1)S(1)} %collective-permute-done.2), channel_id=1, source_target_pairs={{0,4},{4,8},{8,12},{12,16},{16,20},{20,24},{24,28},{28,0},{1,5},{5... | collective-permute-start | bytes 172040 | tf_op jit(solution)/shard_map/ppermute | solution.py:11
  26.3 4.5 %collective-permute-start.4 = (bf16[32,896]{1,0:T(8,128)(2,1)S(1)}, bf16[32,896]{1,0:T(8,128)(2,1)S(1)}, u32[]{:S(2)}, u32[]{:S(2)}) collective-permute-start(bf16[32,896]{1,0:T(8,128)(2,1)S(1)} %collective-permute-done.3), channel_id=1, source_target_pairs={{0,4},{4,8},{8,12},{12,16},{16,20},{20,24},{24,28},{28,0},{1,5},{5... | collective-permute-start | bytes 172040 | tf_op jit(solution)/shard_map/ppermute | solution.py:11
  30.8 5.7 %collective-permute-start.5 = (bf16[32,896]{1,0:T(8,128)(2,1)S(1)}, bf16[32,896]{1,0:T(8,128)(2,1)S(1)}, u32[]{:S(2)}, u32[]{:S(2)}) collective-permute-start(bf16[32,896]{1,0:T(8,128)(2,1)S(1)} %collective-permute-done.4), channel_id=1, source_target_pairs={{0,4},{4,8},{8,12},{12,16},{16,20},{20,24},{24,28},{28,0},{1,5},{5... | collective-permute-start | bytes 172040 | tf_op jit(solution)/shard_map/ppermute | solution.py:11
  36.5 15.5 %collective-permute-start.6 = (bf16[32,896]{1,0:T(8,128)(2,1)S(1)}, bf16[32,896]{1,0:T(8,128)(2,1)S(1)}, u32[]{:S(2)}, u32[]{:S(2)}) collective-permute-start(bf16[32,896]{1,0:T(8,128)(2,1)S(1)} %collective-permute-done.5), channel_id=1, source_target_pairs={{0,4},{4,8},{8,12},{12,16},{16,20},{20,24},{24,28},{28,0},{1,5},{5... | collective-permute-start | bytes 172040 | tf_op jit(solution)/shard_map/ppermute | solution.py:11
  75.9 67.2 %reduce-scatter.7.cloned.1.call-start = ((), (), s32[]{:S(2)}) async-start(), calls=%async_computation.4 | async-start | bytes 1806336
  103.5 2.4 %copy-start = (bf16[112,4,224]{2,1,0:T(4,128)(2,1)S(1)}, bf16[112,4,224]{2,1,0:T(4,128)(2,1)}, u32[]{:S(2)}) copy-start(bf16[112,4,224]{2,1,0:T(4,128)(2,1)} %param.5) | copy-start | bytes 602116
  105.8 38.3 %copy-start.2 = (f32[4]{0:T(128)S(1)}, f32[4]{0:T(128)}, u32[]{:S(2)}) copy-start(f32[4]{0:T(128)} %param.9) | copy-start | bytes 52
Sparse Core Ops, SparseCore 0:
  9.2 30.1 all-gather.1
  76.0 25.9 reduce-scatter.4
  106.0 37.0 reduce-scatter.6
